TPU v7x, 32 devices: a whole 2x2x4 slice. The times are simulated.
32 devices in a mesh: ep: 8 (over z, x), dp: 4 (over y, core).
Axes of the slice: x: 2, y: 2, z: 4, core: 2. Of those that a mesh axis runs over, the one named last changes fastest.
Arguments:
- grad_out: float32 [4096, 1536], P(('ep', 'dp')), may hold values from -6 to 6
- tokens: bfloat16 [4096, 1536], P(('ep', 'dp')), may hold values from -6 to 6
- probs: float32 [4096, 4], P(('ep', 'dp')), may hold values from 0.1 to 0.5
- expert_ids: int32 [4096, 4], P(('ep', 'dp')), may hold values from 0 to 7, all different within a row; in each aligned block of 128 rows (0 to 127, 128 to 255, ...) at most 80 rows name the same one
- priority: int32 [32, 128], P(('ep', 'dp')), may hold values from 0 to 127, each once within a row
- cap_counts: int32 [8], replicated, may hold values from 40 to 80, as said below
- gate_weight: bfloat16 [8, 1536, 1536], P('ep'), may hold values from -0.15625 to 0.15625
- up_weight: bfloat16 [8, 1536, 1536], P('ep'), may hold values from -0.15625 to 0.15625
- down_weight: bfloat16 [8, 1536, 1536], P('ep'), may hold values from -0.15625 to 0.15625
Outputs:
- input_grad: bfloat16 [4096, 1536], P(('ep', 'dp'))
- prob_grad: float32 [4096, 4], P(('ep', 'dp'))
- gate_grad: bfloat16 [8, 1536, 1536], P('ep', 'dp')
- up_grad: bfloat16 [8, 1536, 1536], P('ep', 'dp')
- down_grad: bfloat16 [8, 1536, 1536], P('ep', 'dp')
Inputs may be any that keep to these rules, and one draw needn't show every extreme that they name: `expert_ids`: each row names 4 different experts; among the rows of one device no expert is named by more than 80 rows, and in some device some expert is named by exactly 80 rows. `priority`: each row orders the 128 tokens of one device, each number once. `cap_counts`: some expert has exactly 80.
All inputs are finite; a program needn't handle non-finite values. Where the computation divides by a largest or mean magnitude, that divisor is 1e-20 or more.
Results may differ from a plain program's by a relative error of at most 0.017.
Values may be sent and summed in bfloat16 or wider, within the bound.
A program may use at most 128 MiB of HBM per device.

v0:
```python
import functools

import jax
import jax.numpy as jnp
from jax import lax
from jax.experimental import pallas as pl
from jax.experimental.pallas import tpu as pltpu
from jax.sharding import PartitionSpec as P


sharpness = 1.702


def contract_last(first_op, second_op):
    return lax.dot_general(
        first_op, second_op, (((1,), (1,)), ((), ())), preferred_element_type=jnp.float32
    )


def contract_first(first_op, second_op):
    return lax.dot_general(
        first_op, second_op, (((0,), (0,)), ((), ())), preferred_element_type=jnp.float32
    )


def route_table(expert_ids, priority, cap_counts, buckets, capacity):
    ranking = priority[0]
    earlier = (ranking[None, :] < ranking[:, None]).astype(jnp.bfloat16)
    expert_range = lax.broadcasted_iota(jnp.int32, (1, 1, buckets), 2)
    matches = (expert_ids[:, :, None] == expert_range).astype(jnp.float32)
    routed = jnp.sum(matches, axis=1).astype(jnp.bfloat16)
    before = jnp.dot(earlier, routed, preferred_element_type=jnp.float32)
    slot_rank = jnp.sum(matches * before[:, None, :], axis=2).astype(jnp.int32)
    keep_limit = jnp.sum(matches * cap_counts.astype(jnp.float32)[None, None, :], axis=2)
    kept = slot_rank < keep_limit.astype(jnp.int32)
    return jnp.where(kept, expert_ids * capacity + slot_rank, -1)


def exchange_dispatch(tokens, quantized, pair_weight, placement, ep_size, capacity):
    table = jnp.any(placement, axis=1).astype(jnp.bfloat16)
    bucket_shape = (ep_size, capacity, tokens.shape[1])
    send_x = contract_first(table, tokens).astype(jnp.bfloat16)
    send_q = contract_first(table, quantized).astype(jnp.bfloat16)
    send_weight = jnp.sum(jnp.where(placement, pair_weight[:, :, None], 0.0), axis=(0, 1))
    slot_x = exchange(send_x.reshape(bucket_shape), "ep").reshape(-1, tokens.shape[1])
    slot_q = exchange(send_q.reshape(bucket_shape), "ep").reshape(-1, tokens.shape[1])
    weight = exchange(send_weight.reshape(ep_size, capacity), "ep").reshape(-1)
    return slot_x, slot_q, weight


def relay_dispatch(tokens, quantized, target, pair_weight, capacity):
    ep_size, levels = lax.axis_size("ep"), lax.axis_size("ep") // 2
    me = lax.axis_index("ep")
    z, x = me // 2, me % 2
    meta = jnp.concatenate([target.astype(jnp.float32).T, pair_weight.T], axis=0)
    table = exchange(jnp.broadcast_to(meta[None], (ep_size, *meta.shape)), "ep")
    top = target.shape[1]
    slots = lax.broadcasted_iota(jnp.int32, (1, capacity, 1), 1).astype(jnp.float32)

    def hop(array, step, sign):
        sources = [h for h in range(levels) if 0 <= h - sign * (step - 1) < levels and 0 <= h + sign < levels]
        return lax.ppermute(
            array, "ep", [(2 * h + j, 2 * (h + sign) + j) for h in sources for j in range(2)]
        )

    def hit(block, expert):
        rows = lax.dynamic_index_in_dim(table, block, 0, keepdims=False)[:top]
        base = (expert * capacity).astype(jnp.float32)
        return jnp.any(rows[:, None, :] == slots + base, axis=0).astype(jnp.bfloat16)

    second = jnp.where(z == 0, 1, z - 1)
    third = jnp.where(z < 2, z + 2, z - 2)
    fourth = jnp.where(z == 0, 3, jnp.where(z == 1, 2, jnp.where(z == 2, 3, 0)))
    order = (z, second, third, fourth)
    own_hits = [hit(2 * h + x, me) for h in order]
    cross_hits = [hit(2 * h + x, me ^ 1) for h in order]
    inner = (z == 1) | (z == 2)

    def pick(hits, rows):
        return jnp.dot(hits, rows, preferred_element_type=jnp.float32).astype(jnp.bfloat16)

    def spread(block):
        up_one, down_one = hop(block, 1, 1), hop(block, 1, -1)
        up_two, down_two = hop(up_one, 2, 1), hop(down_one, 2, -1)
        up_three, down_three = hop(up_two, 3, 1), hop(down_two, 3, -1)
        held = (
            block,
            jnp.where(z == 0, down_one, up_one),
            jnp.where(z < 2, down_two, up_two),
            jnp.where(inner, down_one, jnp.where(z == 0, down_three, up_three)),
        )
        out = jnp.zeros((ep_size * capacity, block.shape[1]), jnp.bfloat16)
        for i in range(4):
            crossed = lax.ppermute(
                pick(cross_hits[i], held[i]), "ep", [(d, d ^ 1) for d in range(ep_size)]
            )
            kept_here = pick(own_hits[i], held[i])
            base = 2 * order[i]
            out = lax.dynamic_update_slice_in_dim(out, kept_here, (base + x) * capacity, 0)
            out = lax.dynamic_update_slice_in_dim(out, crossed, (base + 1 - x) * capacity, 0)
        return out, (up_one, down_one)

    slot_x, arrived = spread(tokens)
    quantized, _ = lax.optimization_barrier((quantized, arrived))
    slot_q, _ = spread(quantized)
    targets = table[:, :top, None, :]
    base = (me * capacity).astype(jnp.float32)
    weight = jnp.sum(
        jnp.where(targets == slots[None] + base, table[:, top:, None, :], 0.0), axis=(1, 3)
    )
    return slot_x, slot_q, weight.reshape(-1)


def exchange(array, axis):
    return lax.all_to_all(array, axis, split_axis=0, concat_axis=0, tiled=True)


def pair_scatter(deltas, values, after=None):
    dp_size = lax.axis_size("dp")
    hidden = deltas.shape[1]
    if dp_size != 4:
        part = contract_first(deltas, values).astype(jnp.bfloat16)
        return lax.psum_scatter(part, "dp", scatter_dimension=0, tiled=True), part
    share = hidden // dp_size
    me = lax.axis_index("dp")
    near, far = me ^ 1, me ^ 2

    def quarter(which):
        columns = lax.dynamic_slice_in_dim(deltas, which * share, share, 1)
        return contract_first(columns, values)

    def swap(array, bit):
        return lax.ppermute(array, "dp", [(i, i ^ bit) for i in range(dp_size)])

    from_near_far = swap(quarter(near ^ 2).astype(jnp.bfloat16), 1)
    from_near_own = swap(quarter(near).astype(jnp.bfloat16), 1)
    passed = (quarter(far) + from_near_far.astype(jnp.float32)).astype(jnp.bfloat16)
    from_far = swap(passed, 2)
    if after is not None:
        from_far, _ = lax.optimization_barrier((from_far, after))
    own = quarter(me) + from_near_own.astype(jnp.float32)
    return (own + from_far.astype(jnp.float32)).astype(jnp.bfloat16), passed


def on_device_body(
    grad_out, tokens, probs, expert_ids, priority, cap_counts, gate_weight, up_weight, down_weight
):
    ep_size = lax.axis_size("ep")
    tok_rows, model_width = tokens.shape
    route_count = expert_ids.shape[1]
    capacity = 5 * route_count * tok_rows // (4 * ep_size)
    slot_rows = ep_size * capacity
    bucket_shape = (ep_size, capacity, model_width)
    target = route_table(expert_ids, priority, cap_counts, ep_size, capacity)
    slot_range = lax.broadcasted_iota(jnp.int32, (1, 1, slot_rows), 2)
    placement = target[:, :, None] == slot_range
    row_scale = jnp.maximum(jnp.max(jnp.abs(grad_out), axis=1), 1.0)
    quantized = (grad_out / row_scale[:, None]).astype(jnp.bfloat16)
    pair_weight = probs * row_scale[:, None]
    if ep_size == 8:
        slot_x, slot_q, weight = relay_dispatch(tokens, quantized, target, pair_weight, capacity)
    else:
        slot_x, slot_q, weight = exchange_dispatch(
            tokens, quantized, pair_weight, placement, ep_size, capacity
        )
    weight = weight[:, None]
    w_gate = gate_weight[0]
    w_up = up_weight[0]
    w_down = down_weight[0]

    gate_pre = contract_last(slot_x, w_gate)
    up_pre = contract_last(slot_x, w_up)
    squash = jax.nn.sigmoid(sharpness * gate_pre)
    gated = gate_pre * squash
    activated = (up_pre + 1.0) * gated
    act_scaled = (activated * weight).astype(jnp.bfloat16)
    down_share, passed = pair_scatter(act_scaled, slot_q)
    later_q, _ = lax.optimization_barrier((slot_q, passed))
    back_proj = contract_last(later_q, w_down)
    act_delta = weight * back_proj
    up_delta = (act_delta * gated).astype(jnp.bfloat16)
    gate_delta = (
        act_delta * (up_pre + 1.0) * (squash + sharpness * gate_pre * squash * (1.0 - squash))
    ).astype(jnp.bfloat16)
    slot_out = jnp.sum(activated * back_proj, axis=1)
    gate_share, _ = pair_scatter(gate_delta, slot_x)
    up_share, _ = pair_scatter(up_delta, slot_x, gate_share)
    in_delta = jnp.dot(gate_delta, w_gate, preferred_element_type=jnp.float32) + jnp.dot(
        up_delta, w_up, preferred_element_type=jnp.float32
    )
    slot_in = in_delta.astype(jnp.bfloat16)
    back_in = exchange(slot_in.reshape(bucket_shape), "ep").reshape(slot_rows, model_width)
    back_prob = exchange(slot_out.reshape(ep_size, capacity), "ep").reshape(slot_rows)
    prob_grad = row_scale[:, None] * jnp.sum(
        jnp.where(placement, back_prob[None, None, :], 0.0), axis=2
    )
    table_low = jnp.any(placement, axis=1).astype(jnp.bfloat16)
    input_grad = jnp.dot(table_low, back_in, preferred_element_type=jnp.float32).astype(
        jnp.bfloat16
    )
    return (input_grad, prob_grad, gate_share[None], up_share[None], down_share[None])


MESH = pl.DeviceIdType.MESH


def fused_kernel(
    ep_size, dp_size, capacity, chunk,
    tokens_ref, grad_ref, probs_ref, ids_ref, prio_ref, caps_ref, gate_hbm, up_hbm, down_hbm,
    input_ref, prob_ref, grads_ref,
    w_gate, w_up, w_down, raw, slots, cross, deltas, gated_part, slope_part, act_part, weight_col,
    slot_sum, meta, target_col, scale_col, near_out, far_in, near_in, keep_out, keep_in, result,
    back, prob_out, prob_in,
    load_sem, own_send, relay_send, raw_recv, cross_send, cross_recv, meta_send, meta_recv,
    pass_send, pass_recv, keep_send, keep_recv, far_send, far_recv,
    ret_send, ret_recv, prob_send, prob_recv,
):
    tok_rows, width = tokens_ref.shape
    top = ids_ref.shape[1]
    hidden = w_gate.shape[0]
    share = hidden // dp_size
    chunks = width // chunk
    parts = hidden // chunk
    levels = ep_size // 2
    group = 2 * capacity
    units = 3 * chunks
    me, rep = lax.axis_index("ep"), lax.axis_index("dp")
    z, x = lax.div(me, 2), lax.rem(me, 2)
    partner = me + 1 - 2 * x
    near = rep + 1 - 2 * lax.rem(rep, 2)
    far = lax.rem(rep + 2, dp_size)
    diagonal = lax.rem(near + 2, dp_size)
    high = lax.div(z, 2)
    middle = lax.div(z * (levels - 1 - z), 2)
    end = (levels - 1) * high
    first_target = middle * end + (1 - middle) * (1 + high)
    second_target = 2 - high

    def level_at(place):
        last = lax.div(place, 3)
        inner = lax.rem(place + 1, 3) * (1 - last) + 3 * last
        low = (1 - middle) * place + middle * inner
        return (1 - high) * low + high * (levels - 1 - low)

    def cols(index, size=chunk):
        return pl.ds(pl.multiple_of(index * size, size), size)

    def rows(index, size):
        return pl.ds(pl.multiple_of(index * size, size), size)

    def raw_copy(tensor, level, index, target, sem):
        return pltpu.make_async_remote_copy(
            src_ref=raw.at[tensor, level, index],
            dst_ref=raw.at[tensor, level, index],
            send_sem=sem,
            recv_sem=raw_recv.at[tensor, level, index],
            device_id={"ep": 2 * target + x},
            device_id_type=MESH,
        )

    def own_copy(tensor, which, index):
        target = first_target if which == 0 else second_target
        return raw_copy(tensor, z, index, target, own_send.at[tensor, which, index])

    def relay_copy(tensor, place, index):
        sem = relay_send.at[tensor, lax.div(place, 2), index]
        return raw_copy(tensor, level_at(place), index, end, sem)

    def cross_copy(tensor, level, index):
        return pltpu.make_async_remote_copy(
            src_ref=cross.at[tensor, level, index],
            dst_ref=slots.at[tensor, rows(2 * level + x, capacity), cols(index)],
            send_sem=cross_send.at[tensor, level, index],
            recv_sem=cross_recv.at[tensor, level, index],
            device_id={"ep": partner},
            device_id_type=MESH,
        )

    def meta_copy(step):
        return pltpu.make_async_remote_copy(
            src_ref=meta.at[me],
            dst_ref=meta.at[me],
            send_sem=meta_send.at[step],
            recv_sem=meta_recv.at[me],
            device_id={"ep": lax.rem(me + step, ep_size)},
            device_id_type=MESH,
        )

    def meta_arrival(step):
        source = lax.rem(me + step, ep_size)
        return pltpu.make_async_remote_copy(
            src_ref=meta.at[source],
            dst_ref=meta.at[source],
            send_sem=meta_send.at[step],
            recv_sem=meta_recv.at[source],
            device_id={"ep": source},
            device_id_type=MESH,
        )

    def dp_copy(source, target, send, recv, peer):
        return pltpu.make_async_remote_copy(
            src_ref=source, dst_ref=target, send_sem=send, recv_sem=recv,
            device_id={"dp": peer}, device_id_type=MESH,
        )

    def pass_copy(unit):
        return dp_copy(
            near_out.at[lax.rem(unit, 2)], near_in.at[unit], pass_send.at[unit], pass_recv.at[unit], near
        )

    def keep_copy(unit):
        return dp_copy(
            keep_out.at[lax.rem(unit, 2)], keep_in.at[unit], keep_send.at[unit], keep_recv.at[unit], near
        )

    def far_copy(unit):
        return dp_copy(near_in.at[unit], far_in.at[unit], far_send.at[unit], far_recv.at[unit], far)

    def return_copy(block):
        return pltpu.make_async_remote_copy(
            src_ref=result.at[rows(block, capacity)],
            dst_ref=back.at[rows(me, capacity)],
            send_sem=ret_send.at[block],
            recv_sem=ret_recv.at[me],
            device_id={"ep": block},
            device_id_type=MESH,
        )

    def prob_copy(block):
        return pltpu.make_async_remote_copy(
            src_ref=prob_out.at[block],
            dst_ref=prob_in.at[me],
            send_sem=prob_send.at[block],
            recv_sem=prob_recv.at[me],
            device_id={"ep": block},
            device_id_type=MESH,
        )

    def return_arrival(source):
        return pltpu.make_async_remote_copy(
            src_ref=result.at[rows(source, capacity)],
            dst_ref=back.at[rows(source, capacity)],
            send_sem=ret_send.at[source],
            recv_sem=ret_recv.at[source],
            device_id={"ep": source},
            device_id_type=MESH,
        )

    def prob_arrival(source):
        return pltpu.make_async_remote_copy(
            src_ref=prob_out.at[source],
            dst_ref=prob_in.at[source],
            send_sem=prob_send.at[source],
            recv_sem=prob_recv.at[source],
            device_id={"ep": source},
            device_id_type=MESH,
        )

    loads = [
        pltpu.make_async_copy(source.at[0], target, load_sem.at[i])
        for i, (source, target) in enumerate(((gate_hbm, w_gate), (up_hbm, w_up), (down_hbm, w_down)))
    ]
    for load in loads:
        load.start()
    for index in range(chunks):
        raw[0, z, index] = tokens_ref[:, index * chunk : (index + 1) * chunk]

    barrier = pltpu.get_barrier_semaphore()
    for step in range(1, ep_size):
        pl.semaphore_signal(
            barrier, inc=1, device_id={"ep": lax.rem(me + step, ep_size)}, device_id_type=MESH
        )
    for peer in (near, far):
        pl.semaphore_signal(barrier, inc=1, device_id={"dp": peer}, device_id_type=MESH)
    pl.semaphore_wait(barrier, ep_size + 1)

    for index in range(chunks):
        own_copy(0, 0, index).start()
    scale = jnp.maximum(jnp.max(jnp.abs(grad_ref[...]), axis=1, keepdims=True), 1.0)
    scale_col[...] = scale
    for index in range(chunks):
        piece = grad_ref[:, index * chunk : (index + 1) * chunk]
        raw[1, z, index] = (piece / scale).astype(jnp.bfloat16)
    for index in range(chunks):
        own_copy(1, 0, index).start()
    for tensor in range(2):
        for index in range(chunks):
            own_copy(tensor, 1, index).start()

    square = (tok_rows, tok_rows)
    eye = lax.broadcasted_iota(jnp.int32, square, 0) == lax.broadcasted_iota(jnp.int32, square, 1)
    prio_row = prio_ref[...].astype(jnp.float32)
    prio_col = jnp.sum(jnp.where(eye, prio_row, 0.0), axis=1, keepdims=True)
    earlier = jnp.where(prio_row < prio_col, 1.0, 0.0).astype(jnp.bfloat16)
    lane = lax.broadcasted_iota(jnp.int32, square, 1)
    caps = jnp.zeros((1, tok_rows), jnp.float32)
    for expert in range(ep_size):
        count = caps_ref[expert].astype(jnp.float32)
        caps = caps + jnp.where(lane[:1] == expert, count, 0.0)
    ids = ids_ref[...]
    matches = [jnp.where(ids[:, k : k + 1] == lane, 1.0, 0.0) for k in range(top)]
    routed = sum(matches[1:], matches[0]).astype(jnp.bfloat16)
    before = jnp.dot(earlier, routed, preferred_element_type=jnp.float32)
    pair_weight = probs_ref[...] * scale
    for k in range(top):
        rank = jnp.sum(matches[k] * before, axis=1, keepdims=True)
        limit = jnp.sum(matches[k] * caps, axis=1, keepdims=True)
        place = ids[:, k : k + 1].astype(jnp.float32) * capacity + rank
        target = jnp.where(rank < limit, place, -1.0)
        target_col[k] = target
        meta[me, k : k + 1, :] = jnp.sum(jnp.where(eye, target, 0.0), axis=0, keepdims=True)
        meta[me, top + k : top + k + 1, :] = jnp.sum(
            jnp.where(eye, pair_weight[:, k : k + 1], 0.0), axis=0, keepdims=True
        )
    for step in range(1, ep_size):
        meta_copy(step).start()
    for load in loads:
        load.wait()
    for step in range(1, ep_size):
        meta_arrival(step).wait_recv()

    slot_iota = lax.broadcasted_iota(jnp.int32, (capacity, tok_rows), 0)

    def slot_names(expert):
        return (slot_iota + expert * capacity).astype(jnp.float32)

    def hits(level, expert):
        table, names = meta[2 * level + x], slot_names(expert)
        total = jnp.zeros((capacity, tok_rows), jnp.float32)
        for k in range(top):
            total = total + jnp.where(table[k : k + 1] == names, 1.0, 0.0)
        return total.astype(jnp.bfloat16)

    def event(tensor, place, index):
        level = level_at(place)

        @pl.when(place > 0)
        def _():
            raw_copy(tensor, level, index, end, relay_send.at[tensor, 0, index]).wait_recv()

        @pl.when(middle * lax.rem(place, 2) == 1)
        def _():
            relay_copy(tensor, place, index).start()

        block = raw[tensor, level, index]
        crossed = jnp.dot(hits(level, partner), block, preferred_element_type=jnp.float32)
        cross[tensor, level, index] = crossed.astype(jnp.bfloat16)
        cross_copy(tensor, level, index).start()
        kept = jnp.dot(hits(level, me), block, preferred_element_type=jnp.float32)
        slots[tensor, rows(2 * level + x, capacity), cols(index)] = kept.astype(jnp.bfloat16)

    def forward_part(place, part):
        level = level_at(place)

        @pl.when(part == 0)
        def _():
            for index in range(chunks):
                cross_copy(0, level, index).wait_recv()
            names = slot_names(me)
            for column in range(2):
                table = meta[2 * level + column]
                total = jnp.zeros((capacity, tok_rows), jnp.float32)
                for k in range(top):
                    total = total + jnp.where(
                        table[k : k + 1] == names, table[top + k : top + k + 1], 0.0
                    )
                weight_col[column * capacity : (column + 1) * capacity, :] = jnp.sum(
                    total, axis=1, keepdims=True
                )

        entries = slots[0, rows(level, group), :]
        gate_pre = contract_last(entries, w_gate[rows(part, chunk), :])
        up_one = contract_last(entries, w_up[rows(part, chunk), :]) + 1.0
        squash = jax.nn.sigmoid(sharpness * gate_pre)
        gated = gate_pre * squash
        activated = up_one * gated
        gated_part[part] = gated
        slope_part[part] = up_one * (squash + sharpness * gated * (1.0 - squash))
        act_part[part] = activated
        deltas[0, rows(level, group), cols(part)] = (activated * weight_col[...]).astype(jnp.bfloat16)

    def backward_part(place, part, wait):
        level = level_at(place)
        if wait:

            @pl.when(part == 0)
            def _():
                for index in range(chunks):
                    cross_copy(1, level, index).wait_recv()

        entries = slots[1, rows(level, group), :]
        back_proj = contract_last(entries, w_down[rows(part, chunk), :])
        act_delta = weight_col[...] * back_proj
        deltas[1, rows(level, group), cols(part)] = (act_delta * slope_part[part]).astype(jnp.bfloat16)
        deltas[2, rows(level, group), cols(part)] = (act_delta * gated_part[part]).astype(jnp.bfloat16)
        slot_sum[part] = jnp.sum(act_part[part] * back_proj, axis=1, keepdims=True)

        @pl.when(part == parts - 1)
        def _():
            total = slot_sum[0]
            for other in range(1, parts):
                total = total + slot_sum[other]
            cap_square = (capacity, tok_rows)
            diagonal_mask = lax.broadcasted_iota(jnp.int32, cap_square, 1) == slot_iota
            for column in range(2):
                line = total[column * capacity : (column + 1) * capacity]
                line = jnp.sum(jnp.where(diagonal_mask, line, 0.0), axis=0, keepdims=True)
                prob_out[2 * level + column] = jnp.broadcast_to(line, prob_out.shape[1:])

    def exchange_step(place, carry):
        def token_step(index, inner):
            event(0, place, index)

            @pl.when(place > 0)
            def _():
                backward_part(place - 1, index, True)

            return inner

        def grad_step(index, inner):
            event(1, place, index)
            forward_part(place, index)
            return inner

        lax.fori_loop(0, chunks, token_step, 0)
        lax.fori_loop(0, chunks, grad_step, 0)
        return carry

    lax.fori_loop(0, levels, exchange_step, 0)

    def send_back():
        def level_step(level, carry):
            def column_step(index, inner):
                total = jnp.dot(
                    deltas[1, rows(level, group), :], w_gate[:, cols(index)],
                    preferred_element_type=jnp.float32,
                ) + jnp.dot(
                    deltas[2, rows(level, group), :], w_up[:, cols(index)],
                    preferred_element_type=jnp.float32,
                )
                result[rows(level, group), cols(index)] = total.astype(jnp.bfloat16)
                return inner

            lax.fori_loop(0, chunks, column_step, 0)
            for column in range(2):
                block = 2 * level + column

                @pl.when(block != me)
                def _():
                    return_copy(block).start()
                    prob_copy(block).start()

                @pl.when(block == me)
                def _():
                    back[rows(me, capacity), :] = result[rows(me, capacity), :]
                    prob_in[me] = prob_out[me]

            return carry

        lax.fori_loop(0, levels, level_step, 0)

    def partial_of(unit, quarter):
        tensor, index = lax.div(unit, chunks), lax.rem(unit, chunks)
        values = slots[1 - lax.div(tensor + 1, 2), :, cols(index)]
        return contract_first(deltas[tensor, :, cols(quarter, share)], values)

    def reduce_step(unit, carry):
        @pl.when(unit < chunks)
        def _():
            cross_copy(1, level_at(levels - 1), lax.rem(unit, chunks)).wait_recv()

        @pl.when(unit == chunks)
        def _():
            def last_step(part, inner):
                backward_part(levels - 1, part, False)
                return inner

            lax.fori_loop(0, parts, last_step, 0)

        @pl.when(unit == chunks + 1)
        def _():
            send_back()

        slot = lax.rem(unit, 2)

        @pl.when(unit >= 2)
        def _():
            pass_copy(unit - 2).wait_send()
            keep_copy(unit - 2).wait_send()

        near_out[slot] = partial_of(unit, diagonal).astype(jnp.bfloat16)
        pass_copy(unit).start()
        passed = partial_of(unit, far)
        pass_copy(unit).wait_recv()
        near_in[unit] = (passed + near_in[unit].astype(jnp.float32)).astype(jnp.bfloat16)
        far_copy(unit).start()
        keep_out[slot] = partial_of(unit, near).astype(jnp.bfloat16)
        keep_copy(unit).start()
        return carry

    lax.fori_loop(0, units, reduce_step, 0)

    def combine():
        for step in range(1, ep_size):
            source = lax.rem(me + step, ep_size)
            return_arrival(source).wait_recv()
            prob_arrival(source).wait_recv()
        shape = (tok_rows, ep_size * capacity)
        names = lax.broadcasted_iota(jnp.int32, shape, 1).astype(jnp.float32)
        table = jnp.zeros(shape, jnp.float32)
        for k in range(top):
            table = table + jnp.where(target_col[k] == names, 1.0, 0.0)
        table = table.astype(jnp.bfloat16)
        for index in range(chunks):
            span = slice(index * chunk, (index + 1) * chunk)
            input_ref[:, span] = jnp.dot(
                table, back[:, span], preferred_element_type=jnp.float32
            ).astype(jnp.bfloat16)
        lane_name = lane.astype(jnp.float32)
        for k in range(top):
            total = jnp.zeros((tok_rows, tok_rows), jnp.float32)
            for expert in range(ep_size):
                found = target_col[k] == lane_name + float(expert * capacity)
                total = total + jnp.where(found, prob_in[expert][:1], 0.0)
            prob_ref[:, k : k + 1] = scale_col[...] * jnp.sum(total, axis=1, keepdims=True)

    def finish_step(unit, carry):
        @pl.when(unit == units - 2)
        def _():
            combine()

        total = partial_of(unit, rep)
        keep_copy(unit).wait_recv()
        total = total + keep_in[unit].astype(jnp.float32)
        far_copy(unit).wait_recv()
        tensor, index = lax.div(unit, chunks), lax.rem(unit, chunks)
        grads_ref[tensor, :, cols(index)] = (total + far_in[unit].astype(jnp.float32)).astype(
            jnp.bfloat16
        )
        return carry

    lax.fori_loop(0, units, finish_step, 0)

    for tensor in range(2):
        for index in range(chunks):
            own_copy(tensor, 0, index).wait_send()
            own_copy(tensor, 1, index).wait_send()

            @pl.when(middle == 1)
            def _():
                relay_copy(tensor, 1, index).wait_send()
                relay_copy(tensor, 3, index).wait_send()

            for level in range(levels):
                cross_copy(tensor, level, index).wait_send()
    for step in range(1, ep_size):
        meta_copy(step).wait_send()
        peer = lax.rem(me + step, ep_size)
        return_copy(peer).wait_send()
        prob_copy(peer).wait_send()
    for unit in (units - 2, units - 1):
        pass_copy(unit).wait_send()
        keep_copy(unit).wait_send()
    for unit in range(units):
        far_copy(unit).wait_send()


def fused_body(
    grad_out, tokens, probs, expert_ids, priority, cap_counts, gate_weight, up_weight, down_weight
):
    ep_size, dp_size = lax.axis_size("ep"), lax.axis_size("dp")
    tok_rows, width = tokens.shape
    top = expert_ids.shape[1]
    hidden = gate_weight.shape[1]
    capacity = 5 * top * tok_rows // (4 * ep_size)
    slot_rows = ep_size * capacity
    chunk = width // 3
    chunks, parts, levels = width // chunk, hidden // chunk, ep_size // 2
    share = hidden // dp_size
    units = 3 * chunks
    bf16, f32 = jnp.bfloat16, jnp.float32
    vmem, dma = pltpu.VMEM, pltpu.SemaphoreType.DMA
    in_vmem = pl.BlockSpec(memory_space=pltpu.VMEM)
    anywhere = pl.BlockSpec(memory_space=pl.ANY)
    scratch = [
        vmem((hidden, width), bf16), vmem((hidden, width), bf16), vmem((hidden, width), bf16),
        vmem((2, levels, chunks, tok_rows, chunk), bf16),
        vmem((2, slot_rows, width), bf16),
        vmem((2, levels, chunks, capacity, chunk), bf16),
        vmem((3, slot_rows, hidden), bf16),
        vmem((parts, 2 * capacity, chunk), f32),
        vmem((parts, 2 * capacity, chunk), f32),
        vmem((parts, 2 * capacity, chunk), f32),
        vmem((2 * capacity, 1), f32),
        vmem((parts, 2 * capacity, 1), f32),
        vmem((ep_size, 2 * top, tok_rows), f32),
        vmem((top, tok_rows, 1), f32),
        vmem((tok_rows, 1), f32),
        vmem((2, share, chunk), bf16),
        vmem((units, share, chunk), bf16),
        vmem((units, share, chunk), bf16),
        vmem((2, share, chunk), bf16),
        vmem((units, share, chunk), bf16),
        vmem((slot_rows, width), bf16),
        vmem((slot_rows, width), bf16),
        vmem((ep_size, 8, tok_rows), f32),
        vmem((ep_size, 8, tok_rows), f32),
        dma((3,)), dma((2, 2, chunks)), dma((2, 2, chunks)), dma((2, levels, chunks)),
        dma((2, levels, chunks)), dma((2, levels, chunks)), dma((ep_size,)), dma((ep_size,)),
        dma((units,)), dma((units,)), dma((units,)), dma((units,)), dma((units,)), dma((units,)),
        dma((ep_size,)), dma((ep_size,)), dma((ep_size,)), dma((ep_size,)),
    ]
    input_grad, prob_grad, grads = pl.pallas_call(
        functools.partial(fused_kernel, ep_size, dp_size, capacity, chunk),
        out_shape=(
            jax.ShapeDtypeStruct((tok_rows, width), bf16),
            jax.ShapeDtypeStruct((tok_rows, top), f32),
            jax.ShapeDtypeStruct((3, share, width), bf16),
        ),
        in_specs=[in_vmem] * 5 + [pl.BlockSpec(memory_space=pltpu.SMEM)] + [anywhere] * 3,
        out_specs=(in_vmem, in_vmem, in_vmem),
        scratch_shapes=scratch,
        compiler_params=pltpu.CompilerParams(
            collective_id=0, has_side_effects=True, vmem_limit_bytes=66_000_000
        ),
        name="fused_step",
    )(tokens, grad_out, probs, expert_ids, priority, cap_counts, gate_weight, up_weight, down_weight)
    return input_grad, prob_grad, grads[1][None], grads[2][None], grads[0][None]


def on_device(*arrays):
    return on_device_body(*arrays)


def solution(mesh):
    fused = mesh.shape["ep"] == 8 and mesh.shape["dp"] == 4
    return jax.shard_map(
        fused_body if fused else on_device,
        mesh=mesh,
        in_specs=(
            P(("ep", "dp"), None),
            P(("ep", "dp"), None),
            P(("ep", "dp"), None),
            P(("ep", "dp"), None),
            P(("ep", "dp"), None),
            P(),
            P("ep", None, None),
            P("ep", None, None),
            P("ep", None, None),
        ),
        out_specs=(
            P(("ep", "dp"), None),
            P(("ep", "dp"), None),
            P("ep", "dp", None),
            P("ep", "dp", None),
            P("ep", "dp", None),
        ),
        check_vma=False,
    )
```

profile of v0, /device:TPU:4, one launch (start us, length us, event | category | flops | bytes accessed | tf_op | source)
XLA Modules:
  0.0 191.5 jit_solution(14138494647789134584)
XLA Ops:
  0.6 1.4 copy.14.probs_ref
  2.0 1.4 copy.15.ids_ref
  3.5 181.9 %fused_step.1 = (bf16[128,1536]{1,0:T(8,128)(2,1)}, f32[128,4]{1,0:T(8,128)}, bf16[3,384,1536]{2,1,0:T(8,128)(2,1)}) custom-call(bf16[128,1536]{1,0:T(8,128)(2,1)} %tokens_ref.1, f32[128,1536]{1,0:T(8,128)} %grad_ref.1, f32[128,4]{1,0:T(8,128)} %copy.14.probs_ref, s32[128,4]{1,0:T(8,128)} %copy.15.ids_ref, s32[1,128]{1,0:T(1,128)} %prio_ref.1, s32[8]{0:T(128)} %caps_ref.1, ...), custom_call_target="tpu_custom_call" | custom-call | tf_op jit(solution)/shard_map/fused_step/pallas_call | solution.py:713
  185.4 1.5 copy.16
  186.9 0.0 copy-start
  186.9 3.9 %fusion = (bf16[1,384,1536]{2,1,0:T(8,128)(2,1)}, bf16[1,384,1536]{2,1,0:T(8,128)(2,1)}, bf16[1,384,1536]{2,1,0:T(8,128)(2,1)}) fusion(bf16[3,384,1536]{2,1,0:T(8,128)(2,1)} %get-tuple-element.10), kind=kLoop, calls=%fused_computation | loop fusion | bytes 7077888 | tf_op jit(solution)/shard_map/slice | solution.py:728
  190.8 0.0 copy-done
  190.8 0.7 copy.18
Async XLA Ops:
  186.9 3.9 %copy-start = (bf16[128,1536]{1,0:T(8,128)(2,1)S(1)}, bf16[128,1536]{1,0:T(8,128)(2,1)}, u32[]{:S(2)}) copy-start(bf16[128,1536]{1,0:T(8,128)(2,1)} %get-tuple-element.24) | copy-start | bytes 1179652
where the time goes:
time: 194 us; the launch traced here: 192 us
  Pallas kernels  182 us (94%)
  local copies, waits for them, and re-layouts  8.97 us (5%)
    pallas_call x1, Pallas kernels, fused_body(): pl.pallas_call(functools.partial(fused_kernel, ep_size, dp_size, capacity...  182 us
    unnamed x6, local copies, waits for them, and re-layouts  5.07 us
    slice x1, local copies, waits for them, and re-layouts, fused_body(): grads[0][None]  3.9 us

commit v1 on v0

--- a/solution.py
+++ b/solution.py
@@ -216,7 +216,7 @@
     ret_send, ret_recv, prob_send, prob_recv,
 ):
     tok_rows, width = tokens_ref.shape
-    top = ids_ref.shape[1]
+    top = ids_ref.shape[0]
     hidden = w_gate.shape[0]
     share = hidden // dp_size
     chunks = width // chunk
@@ -374,46 +374,47 @@
         pl.semaphore_signal(barrier, inc=1, device_id={"dp": peer}, device_id_type=MESH)
     pl.semaphore_wait(barrier, ep_size + 1)
 
-    for index in range(chunks):
-        own_copy(0, 0, index).start()
+    own_copy(0, 0, 0).start()
     scale = jnp.maximum(jnp.max(jnp.abs(grad_ref[...]), axis=1, keepdims=True), 1.0)
     scale_col[...] = scale
+    square = (tok_rows, tok_rows)
+    eye = lax.broadcasted_iota(jnp.int32, square, 0) == lax.broadcasted_iota(jnp.int32, square, 1)
+
+    def as_row(column):
+        return jnp.sum(jnp.where(eye, column, 0.0), axis=0, keepdims=True)
+
+    def as_column(row):
+        return jnp.sum(jnp.where(eye, row, 0.0), axis=1, keepdims=True)
+
+    prio_row = prio_ref[...].astype(jnp.float32)
+    earlier = jnp.where(as_column(prio_row) < prio_row, 1.0, 0.0).astype(jnp.bfloat16)
+    expert_iota = lax.broadcasted_iota(jnp.int32, (ep_size, tok_rows), 0)
+    caps = jnp.zeros((ep_size, tok_rows), jnp.float32)
+    for expert in range(ep_size):
+        caps = jnp.where(expert_iota == expert, caps_ref[expert].astype(jnp.float32), caps)
+    matches = [jnp.where(ids_ref[k : k + 1, :] == expert_iota, 1.0, 0.0) for k in range(top)]
+    routed = sum(matches[1:], matches[0]).astype(jnp.bfloat16)
+    before = jnp.dot(routed, earlier, preferred_element_type=jnp.float32)
+    scale_row = as_row(scale)
+    for k in range(top):
+        rank = jnp.sum(matches[k] * before, axis=0, keepdims=True)
+        limit = jnp.sum(matches[k] * caps, axis=0, keepdims=True)
+        place = ids_ref[k : k + 1, :].astype(jnp.float32) * capacity + rank
+        meta[me, k : k + 1, :] = jnp.where(rank < limit, place, -1.0)
+        meta[me, top + k : top + k + 1, :] = probs_ref[k : k + 1, :] * scale_row
+    for step in range(1, ep_size):
+        meta_copy(step).start()
+    for index in range(1, chunks):
+        own_copy(0, 0, index).start()
     for index in range(chunks):
         piece = grad_ref[:, index * chunk : (index + 1) * chunk]
         raw[1, z, index] = (piece / scale).astype(jnp.bfloat16)
-    for index in range(chunks):
         own_copy(1, 0, index).start()
     for tensor in range(2):
         for index in range(chunks):
             own_copy(tensor, 1, index).start()
-
-    square = (tok_rows, tok_rows)
-    eye = lax.broadcasted_iota(jnp.int32, square, 0) == lax.broadcasted_iota(jnp.int32, square, 1)
-    prio_row = prio_ref[...].astype(jnp.float32)
-    prio_col = jnp.sum(jnp.where(eye, prio_row, 0.0), axis=1, keepdims=True)
-    earlier = jnp.where(prio_row < prio_col, 1.0, 0.0).astype(jnp.bfloat16)
-    lane = lax.broadcasted_iota(jnp.int32, square, 1)
-    caps = jnp.zeros((1, tok_rows), jnp.float32)
-    for expert in range(ep_size):
-        count = caps_ref[expert].astype(jnp.float32)
-        caps = caps + jnp.where(lane[:1] == expert, count, 0.0)
-    ids = ids_ref[...]
-    matches = [jnp.where(ids[:, k : k + 1] == lane, 1.0, 0.0) for k in range(top)]
-    routed = sum(matches[1:], matches[0]).astype(jnp.bfloat16)
-    before = jnp.dot(earlier, routed, preferred_element_type=jnp.float32)
-    pair_weight = probs_ref[...] * scale
     for k in range(top):
-        rank = jnp.sum(matches[k] * before, axis=1, keepdims=True)
-        limit = jnp.sum(matches[k] * caps, axis=1, keepdims=True)
-        place = ids[:, k : k + 1].astype(jnp.float32) * capacity + rank
-        target = jnp.where(rank < limit, place, -1.0)
-        target_col[k] = target
-        meta[me, k : k + 1, :] = jnp.sum(jnp.where(eye, target, 0.0), axis=0, keepdims=True)
-        meta[me, top + k : top + k + 1, :] = jnp.sum(
-            jnp.where(eye, pair_weight[:, k : k + 1], 0.0), axis=0, keepdims=True
-        )
-    for step in range(1, ep_size):
-        meta_copy(step).start()
+        target_col[k] = as_column(meta[me, k : k + 1, :])
     for load in loads:
         load.wait()
     for step in range(1, ep_size):
@@ -616,13 +617,13 @@
             input_ref[:, span] = jnp.dot(
                 table, back[:, span], preferred_element_type=jnp.float32
             ).astype(jnp.bfloat16)
-        lane_name = lane.astype(jnp.float32)
+        lane_name = lax.broadcasted_iota(jnp.int32, square, 1).astype(jnp.float32)
         for k in range(top):
             total = jnp.zeros((tok_rows, tok_rows), jnp.float32)
             for expert in range(ep_size):
                 found = target_col[k] == lane_name + float(expert * capacity)
                 total = total + jnp.where(found, prob_in[expert][:1], 0.0)
-            prob_ref[:, k : k + 1] = scale_col[...] * jnp.sum(total, axis=1, keepdims=True)
+            prob_ref[k : k + 1, :] = as_row(scale_col[...] * jnp.sum(total, axis=1, keepdims=True))
 
     def finish_step(unit, carry):
         @pl.when(unit == units - 2)
@@ -714,7 +715,7 @@
         functools.partial(fused_kernel, ep_size, dp_size, capacity, chunk),
         out_shape=(
             jax.ShapeDtypeStruct((tok_rows, width), bf16),
-            jax.ShapeDtypeStruct((tok_rows, top), f32),
+            jax.ShapeDtypeStruct((top, tok_rows), f32),
             jax.ShapeDtypeStruct((3, share, width), bf16),
         ),
         in_specs=[in_vmem] * 5 + [pl.BlockSpec(memory_space=pltpu.SMEM)] + [anywhere] * 3,
@@ -724,8 +725,10 @@
             collective_id=0, has_side_effects=True, vmem_limit_bytes=66_000_000
         ),
         name="fused_step",
-    )(tokens, grad_out, probs, expert_ids, priority, cap_counts, gate_weight, up_weight, down_weight)
-    return input_grad, prob_grad, grads[1][None], grads[2][None], grads[0][None]
+    )(
+        tokens, grad_out, probs.T, expert_ids.T, priority, cap_counts, gate_weight, up_weight, down_weight
+    )
+    return input_grad, prob_grad.T, grads[1][None], grads[2][None], grads[0][None]
 
 
 def on_device(*arrays):

time: 194 us -> 164 us (0.85)
  Pallas kernels: 182 us -> 155 us
  local copies, waits for them, and re-layouts: 8.97 us -> 5.23 us
    pallas_call x1, Pallas kernels: 182 us -> 155 us  [fused_body(): pl.pallas_call(functools.partial(fused_kernel, ep_size, dp_size, capacity...]
    unnamed x6, local copies, waits for them, and re-layouts: 5.07 us -> 1.33 us
where the time goes in v1:
time: 164 us; the launch traced here: 161 us
  Pallas kernels  155 us (95%)
  local copies, waits for them, and re-layouts  5.23 us (3%)
    pallas_call x1, Pallas kernels, fused_body(): pl.pallas_call(functools.partial(fused_kernel, ep_size, dp_size, capacity...  155 us
    slice x1, local copies, waits for them, and re-layouts, fused_body(): grads[0][None]  3.9 us

profile of v1, /device:TPU:4, one launch (start us, length us, event | category | flops | bytes accessed | tf_op | source)
XLA Modules:
  0.0 160.8 jit_solution(13149740581282861627)
XLA Ops:
  0.6 154.9 %fused_step.1 = (bf16[128,1536]{1,0:T(8,128)(2,1)}, f32[4,128]{1,0:T(4,128)}, bf16[3,384,1536]{2,1,0:T(8,128)(2,1)}) custom-call(bf16[128,1536]{1,0:T(8,128)(2,1)} %tokens_ref.1, f32[128,1536]{1,0:T(8,128)} %grad_ref.1, f32[4,128]{1,0:T(4,128)} %bitcast.3, s32[4,128]{1,0:T(4,128)} %bitcast.4, s32[1,128]{1,0:T(1,128)} %prio_ref.1, s32[8]{0:T(128)} %caps_ref.1, ...), custom_call_target="tpu_custom_call" | custom-call | tf_op jit(solution)/shard_map/fused_step/pallas_call | solution.py:714
  155.6 0.0 copy-start
  155.6 0.0 copy-start.1
  155.6 3.9 %fusion = (bf16[1,384,1536]{2,1,0:T(8,128)(2,1)}, bf16[1,384,1536]{2,1,0:T(8,128)(2,1)}, bf16[1,384,1536]{2,1,0:T(8,128)(2,1)}) fusion(bf16[3,384,1536]{2,1,0:T(8,128)(2,1)} %get-tuple-element.10), kind=kLoop, calls=%fused_computation | loop fusion | bytes 7077888 | tf_op jit(solution)/shard_map/slice | solution.py:731
  159.5 0.0 copy-done
  159.5 0.7 copy.16
  160.3 0.0 copy-done.1
  160.3 0.6 copy.17
Async XLA Ops:
  155.6 3.9 %copy-start = (bf16[128,1536]{1,0:T(8,128)(2,1)S(1)}, bf16[128,1536]{1,0:T(8,128)(2,1)}, u32[]{:S(2)}) copy-start(bf16[128,1536]{1,0:T(8,128)(2,1)} %get-tuple-element.19) | copy-start | bytes 1179652
  155.6 4.7 %copy-start.1 = (f32[4,128]{1,0:T(4,128)S(1)}, f32[4,128]{1,0:T(4,128)}, u32[]{:S(2)}) copy-start(f32[4,128]{1,0:T(4,128)} %get-tuple-element.9) | copy-start | bytes 6148

commit v2 on v1

--- a/solution.py
+++ b/solution.py
@@ -208,22 +208,22 @@
     ep_size, dp_size, capacity, chunk,
     tokens_ref, grad_ref, probs_ref, ids_ref, prio_ref, caps_ref, gate_hbm, up_hbm, down_hbm,
     input_ref, prob_ref, grads_ref,
-    w_gate, w_up, w_down, raw, slots, cross, deltas, gated_part, slope_part, act_part, weight_col,
-    slot_sum, meta, target_col, scale_col, near_out, far_in, near_in, keep_out, keep_in, result,
-    back, prob_out, prob_in,
+    w_gate, w_up, w_down, raw, slots, cross, deltas, act_part, weight_col,
+    slot_sum, meta, target_col, scale_col, keep_out, keep_in, result, back, prob_out, prob_in,
+    far_slots, far_deltas, far_weight, far_meta,
     load_sem, own_send, relay_send, raw_recv, cross_send, cross_recv, meta_send, meta_recv,
-    pass_send, pass_recv, keep_send, keep_recv, far_send, far_recv,
-    ret_send, ret_recv, prob_send, prob_recv,
+    keep_send, keep_recv, ret_send, ret_recv, prob_send, prob_recv,
+    slot_send, slot_recv, side_send, side_recv, table_send, table_recv,
 ):
     tok_rows, width = tokens_ref.shape
     top = ids_ref.shape[0]
     hidden = w_gate.shape[0]
     share = hidden // dp_size
     chunks = width // chunk
-    parts = hidden // chunk
     levels = ep_size // 2
     group = 2 * capacity
-    units = 3 * chunks
+    pair = 2 * group
+    units = 3
     me, rep = lax.axis_index("ep"), lax.axis_index("dp")
     z, x = lax.div(me, 2), lax.rem(me, 2)
     partner = me + 1 - 2 * x
@@ -248,15 +248,15 @@
     def rows(index, size):
         return pl.ds(pl.multiple_of(index * size, size), size)
 
+    def remote(source, target, send, recv, peer):
+        return pltpu.make_async_remote_copy(
+            src_ref=source, dst_ref=target, send_sem=send, recv_sem=recv,
+            device_id=peer, device_id_type=MESH,
+        )
+
     def raw_copy(tensor, level, index, target, sem):
-        return pltpu.make_async_remote_copy(
-            src_ref=raw.at[tensor, level, index],
-            dst_ref=raw.at[tensor, level, index],
-            send_sem=sem,
-            recv_sem=raw_recv.at[tensor, level, index],
-            device_id={"ep": 2 * target + x},
-            device_id_type=MESH,
-        )
+        block = raw.at[tensor, level, index]
+        return remote(block, block, sem, raw_recv.at[tensor, level, index], {"ep": 2 * target + x})
 
     def own_copy(tensor, which, index):
         target = first_target if which == 0 else second_target
@@ -266,95 +266,74 @@
         sem = relay_send.at[tensor, lax.div(place, 2), index]
         return raw_copy(tensor, level_at(place), index, end, sem)
 
-    def cross_copy(tensor, level, index):
-        return pltpu.make_async_remote_copy(
-            src_ref=cross.at[tensor, level, index],
-            dst_ref=slots.at[tensor, rows(2 * level + x, capacity), cols(index)],
-            send_sem=cross_send.at[tensor, level, index],
-            recv_sem=cross_recv.at[tensor, level, index],
-            device_id={"ep": partner},
-            device_id_type=MESH,
+    def cross_copy(tensor, place, index):
+        return remote(
+            cross.at[tensor, lax.rem(place, 2), index],
+            slots.at[tensor, rows(2 * place + x, capacity), cols(index)],
+            cross_send.at[tensor, place, index], cross_recv.at[tensor, place, index],
+            {"ep": partner},
         )
 
     def meta_copy(step):
-        return pltpu.make_async_remote_copy(
-            src_ref=meta.at[me],
-            dst_ref=meta.at[me],
-            send_sem=meta_send.at[step],
-            recv_sem=meta_recv.at[me],
-            device_id={"ep": lax.rem(me + step, ep_size)},
-            device_id_type=MESH,
-        )
+        peer = lax.rem(me + step, ep_size)
+        return remote(meta.at[me], meta.at[me], meta_send.at[step], meta_recv.at[me], {"ep": peer})
 
     def meta_arrival(step):
-        source = lax.rem(me + step, ep_size)
-        return pltpu.make_async_remote_copy(
-            src_ref=meta.at[source],
-            dst_ref=meta.at[source],
-            send_sem=meta_send.at[step],
-            recv_sem=meta_recv.at[source],
-            device_id={"ep": source},
-            device_id_type=MESH,
-        )
-
-    def dp_copy(source, target, send, recv, peer):
-        return pltpu.make_async_remote_copy(
-            src_ref=source, dst_ref=target, send_sem=send, recv_sem=recv,
-            device_id={"dp": peer}, device_id_type=MESH,
-        )
-
-    def pass_copy(unit):
-        return dp_copy(
-            near_out.at[lax.rem(unit, 2)], near_in.at[unit], pass_send.at[unit], pass_recv.at[unit], near
+        peer = lax.rem(me + step, ep_size)
+        table = meta.at[peer]
+        return remote(table, table, meta_send.at[step], meta_recv.at[peer], {"ep": peer})
+
+    def table_copy(which):
+        peer = far if which == 0 else diagonal
+        return remote(
+            meta, far_meta.at[which], table_send.at[which], table_recv.at[which], {"dp": peer}
         )
 
     def keep_copy(unit):
-        return dp_copy(
-            keep_out.at[lax.rem(unit, 2)], keep_in.at[unit], keep_send.at[unit], keep_recv.at[unit], near
-        )
-
-    def far_copy(unit):
-        return dp_copy(near_in.at[unit], far_in.at[unit], far_send.at[unit], far_recv.at[unit], far)
-
-    def return_copy(block):
-        return pltpu.make_async_remote_copy(
-            src_ref=result.at[rows(block, capacity)],
-            dst_ref=back.at[rows(me, capacity)],
-            send_sem=ret_send.at[block],
-            recv_sem=ret_recv.at[me],
-            device_id={"ep": block},
-            device_id_type=MESH,
-        )
-
-    def prob_copy(block):
-        return pltpu.make_async_remote_copy(
-            src_ref=prob_out.at[block],
-            dst_ref=prob_in.at[me],
-            send_sem=prob_send.at[block],
-            recv_sem=prob_recv.at[me],
-            device_id={"ep": block},
-            device_id_type=MESH,
+        return remote(
+            keep_out, keep_in.at[unit], keep_send.at[unit], keep_recv.at[unit],
+            {"dp": near},
+        )
+
+    def far_rows(place, which):
+        return pl.ds(pl.multiple_of(which * pair + lax.rem(place, 2) * group, group), group)
+
+    def slot_copy(tensor, place, column):
+        start = lax.rem(place, 2) * group + column * capacity
+        return remote(
+            slots.at[tensor, rows(2 * place + column, capacity)],
+            far_slots.at[
+                tensor, lax.div(place, 2), pl.ds(pl.multiple_of(start, capacity), capacity)
+            ],
+            slot_send.at[tensor, place, column], slot_recv.at[tensor, place, column], {"dp": far},
+        )
+
+    def side_copy(tensor, place):
+        return remote(
+            far_slots.at[tensor, lax.div(place, 2), far_rows(place, 0)],
+            far_slots.at[tensor, lax.div(place, 2), far_rows(place, 1)],
+            side_send.at[tensor, place], side_recv.at[tensor, place], {"dp": near},
+        )
+
+    def return_copy(place, column, block):
+        return remote(
+            result.at[rows(2 * place + column, capacity)], back.at[rows(me, capacity)],
+            ret_send.at[place, column], ret_recv.at[me], {"ep": block},
+        )
+
+    def prob_copy(place, column, block):
+        return remote(
+            prob_out.at[place, column], prob_in.at[me],
+            prob_send.at[place, column], prob_recv.at[me], {"ep": block},
         )
 
     def return_arrival(source):
-        return pltpu.make_async_remote_copy(
-            src_ref=result.at[rows(source, capacity)],
-            dst_ref=back.at[rows(source, capacity)],
-            send_sem=ret_send.at[source],
-            recv_sem=ret_recv.at[source],
-            device_id={"ep": source},
-            device_id_type=MESH,
-        )
+        span = back.at[rows(source, capacity)]
+        return remote(span, span, ret_send.at[0, 0], ret_recv.at[source], {"ep": source})
 
     def prob_arrival(source):
-        return pltpu.make_async_remote_copy(
-            src_ref=prob_out.at[source],
-            dst_ref=prob_in.at[source],
-            send_sem=prob_send.at[source],
-            recv_sem=prob_recv.at[source],
-            device_id={"ep": source},
-            device_id_type=MESH,
-        )
+        span = prob_in.at[source]
+        return remote(span, span, prob_send.at[0, 0], prob_recv.at[source], {"ep": source})
 
     loads = [
         pltpu.make_async_copy(source.at[0], target, load_sem.at[i])
@@ -370,9 +349,9 @@
         pl.semaphore_signal(
             barrier, inc=1, device_id={"ep": lax.rem(me + step, ep_size)}, device_id_type=MESH
         )
-    for peer in (near, far):
+    for peer in (near, far, diagonal):
         pl.semaphore_signal(barrier, inc=1, device_id={"dp": peer}, device_id_type=MESH)
-    pl.semaphore_wait(barrier, ep_size + 1)
+    pl.semaphore_wait(barrier, ep_size + 2)
 
     own_copy(0, 0, 0).start()
     scale = jnp.maximum(jnp.max(jnp.abs(grad_ref[...]), axis=1, keepdims=True), 1.0)
@@ -415,10 +394,6 @@
             own_copy(tensor, 1, index).start()
     for k in range(top):
         target_col[k] = as_column(meta[me, k : k + 1, :])
-    for load in loads:
-        load.wait()
-    for step in range(1, ep_size):
-        meta_arrival(step).wait_recv()
 
     slot_iota = lax.broadcasted_iota(jnp.int32, (capacity, tok_rows), 0)
 
@@ -432,6 +407,13 @@
             total = total + jnp.where(table[k : k + 1] == names, 1.0, 0.0)
         return total.astype(jnp.bfloat16)
 
+    def weight_of(table):
+        names = slot_names(me)
+        total = jnp.zeros((capacity, tok_rows), jnp.float32)
+        for k in range(top):
+            total = total + jnp.where(table[k : k + 1] == names, table[top + k : top + k + 1], 0.0)
+        return jnp.sum(total, axis=1, keepdims=True)
+
     def event(tensor, place, index):
         level = level_at(place)
 
@@ -443,163 +425,189 @@
         def _():
             relay_copy(tensor, place, index).start()
 
+        @pl.when(place > 1)
+        def _():
+            cross_copy(tensor, place - 2, index).wait_send()
+
         block = raw[tensor, level, index]
         crossed = jnp.dot(hits(level, partner), block, preferred_element_type=jnp.float32)
-        cross[tensor, level, index] = crossed.astype(jnp.bfloat16)
-        cross_copy(tensor, level, index).start()
+        cross[tensor, lax.rem(place, 2), index] = crossed.astype(jnp.bfloat16)
+        cross_copy(tensor, place, index).start()
         kept = jnp.dot(hits(level, me), block, preferred_element_type=jnp.float32)
-        slots[tensor, rows(2 * level + x, capacity), cols(index)] = kept.astype(jnp.bfloat16)
-
-    def forward_part(place, part):
-        level = level_at(place)
-
-        @pl.when(part == 0)
-        def _():
-            for index in range(chunks):
-                cross_copy(0, level, index).wait_recv()
-            names = slot_names(me)
-            for column in range(2):
-                table = meta[2 * level + column]
-                total = jnp.zeros((capacity, tok_rows), jnp.float32)
-                for k in range(top):
-                    total = total + jnp.where(
-                        table[k : k + 1] == names, table[top + k : top + k + 1], 0.0
-                    )
-                weight_col[column * capacity : (column + 1) * capacity, :] = jnp.sum(
-                    total, axis=1, keepdims=True
-                )
-
-        entries = slots[0, rows(level, group), :]
-        gate_pre = contract_last(entries, w_gate[rows(part, chunk), :])
-        up_one = contract_last(entries, w_up[rows(part, chunk), :]) + 1.0
+        slots[tensor, rows(2 * place + x, capacity), cols(index)] = kept.astype(jnp.bfloat16)
+
+        @pl.when(index == chunks - 1)
+        def _():
+            slot_copy(tensor, place, x).start()
+
+    def share_slots(tensor, place):
+        for index in range(chunks):
+            cross_copy(tensor, place, index).wait_recv()
+        slot_copy(tensor, place, 1 - x).start()
+
+    def activate(gate_pre, up_pre):
+        up_one = up_pre + 1.0
         squash = jax.nn.sigmoid(sharpness * gate_pre)
         gated = gate_pre * squash
-        activated = up_one * gated
-        gated_part[part] = gated
-        slope_part[part] = up_one * (squash + sharpness * gated * (1.0 - squash))
-        act_part[part] = activated
-        deltas[0, rows(level, group), cols(part)] = (activated * weight_col[...]).astype(jnp.bfloat16)
-
-    def backward_part(place, part, wait):
-        level = level_at(place)
-        if wait:
-
-            @pl.when(part == 0)
-            def _():
-                for index in range(chunks):
-                    cross_copy(1, level, index).wait_recv()
-
-        entries = slots[1, rows(level, group), :]
-        back_proj = contract_last(entries, w_down[rows(part, chunk), :])
-        act_delta = weight_col[...] * back_proj
-        deltas[1, rows(level, group), cols(part)] = (act_delta * slope_part[part]).astype(jnp.bfloat16)
-        deltas[2, rows(level, group), cols(part)] = (act_delta * gated_part[part]).astype(jnp.bfloat16)
-        slot_sum[part] = jnp.sum(act_part[part] * back_proj, axis=1, keepdims=True)
-
-        @pl.when(part == parts - 1)
-        def _():
-            total = slot_sum[0]
-            for other in range(1, parts):
-                total = total + slot_sum[other]
+        return gated, up_one * (squash + sharpness * gated * (1.0 - squash)), up_one * gated
+
+    def forward_part(first, count, part):
+        @pl.when(part == 0)
+        def _():
+            for inner in range(count):
+                for column in range(2):
+                    base = inner * group + column * capacity
+                    table = meta[2 * level_at(first + inner) + column]
+                    weight_col[base : base + capacity, :] = weight_of(table)
+
+        size = count * group
+        span = pl.ds(pl.multiple_of(first * group, group), size)
+        entries = slots[0, span, :]
+        gate_pre = contract_last(entries, w_gate[rows(part, chunk), :])
+        up_pre = contract_last(entries, w_up[rows(part, chunk), :])
+        gated, slope, activated = activate(gate_pre, up_pre)
+        deltas[1, span, cols(part)] = slope.astype(jnp.bfloat16)
+        deltas[2, span, cols(part)] = gated.astype(jnp.bfloat16)
+        act_part[part, :size] = activated.astype(jnp.bfloat16)
+        deltas[0, span, cols(part)] = (activated * weight_col[:size]).astype(jnp.bfloat16)
+
+    def backward_part(first, count, part):
+        size = count * group
+        span = pl.ds(pl.multiple_of(first * group, group), size)
+        back_proj = contract_last(slots[1, span, :], w_down[rows(part, chunk), :])
+        act_delta = weight_col[:size] * back_proj
+        for kind in (1, 2):
+            stored = deltas[kind, span, cols(part)]
+            deltas[kind, span, cols(part)] = (act_delta * stored).astype(jnp.bfloat16)
+        slot_sum[part, :size] = jnp.sum(act_part[part, :size] * back_proj, axis=1, keepdims=True)
+
+        @pl.when(part == chunks - 1)
+        def _():
+            total = slot_sum[0, :size]
+            for other in range(1, chunks):
+                total = total + slot_sum[other, :size]
             cap_square = (capacity, tok_rows)
-            diagonal_mask = lax.broadcasted_iota(jnp.int32, cap_square, 1) == slot_iota
+            mask = lax.broadcasted_iota(jnp.int32, cap_square, 1) == slot_iota
+            for inner in range(count):
+                for column in range(2):
+                    base = inner * group + column * capacity
+                    line = jnp.sum(
+                        jnp.where(mask, total[base : base + capacity], 0.0), axis=0, keepdims=True
+                    )
+                    prob_out[first + inner, column] = jnp.broadcast_to(line, prob_out.shape[2:])
+
+    def return_part(first, count, part):
+        span = pl.ds(pl.multiple_of(first * group, group), count * group)
+        total = jnp.dot(
+            deltas[1, span, :], w_gate[:, cols(part)], preferred_element_type=jnp.float32
+        ) + jnp.dot(deltas[2, span, :], w_up[:, cols(part)], preferred_element_type=jnp.float32)
+        result[span, cols(part)] = total.astype(jnp.bfloat16)
+
+        @pl.when((part == chunks - 1) & ((first == 0) | (middle == 0)))
+        def _():
+            send_back(first, count)
+
+    def send_back(first, count):
+        for inner in range(count):
+            place = first + count - 1 - inner
             for column in range(2):
-                line = total[column * capacity : (column + 1) * capacity]
-                line = jnp.sum(jnp.where(diagonal_mask, line, 0.0), axis=0, keepdims=True)
-                prob_out[2 * level + column] = jnp.broadcast_to(line, prob_out.shape[1:])
-
-    def exchange_step(place, carry):
-        def token_step(index, inner):
-            event(0, place, index)
-
-            @pl.when(place > 0)
-            def _():
-                backward_part(place - 1, index, True)
-
-            return inner
-
-        def grad_step(index, inner):
-            event(1, place, index)
-            forward_part(place, index)
-            return inner
-
-        lax.fori_loop(0, chunks, token_step, 0)
-        lax.fori_loop(0, chunks, grad_step, 0)
-        return carry
-
-    lax.fori_loop(0, levels, exchange_step, 0)
-
-    def send_back():
-        def level_step(level, carry):
-            def column_step(index, inner):
-                total = jnp.dot(
-                    deltas[1, rows(level, group), :], w_gate[:, cols(index)],
-                    preferred_element_type=jnp.float32,
-                ) + jnp.dot(
-                    deltas[2, rows(level, group), :], w_up[:, cols(index)],
-                    preferred_element_type=jnp.float32,
-                )
-                result[rows(level, group), cols(index)] = total.astype(jnp.bfloat16)
-                return inner
-
-            lax.fori_loop(0, chunks, column_step, 0)
-            for column in range(2):
-                block = 2 * level + column
+                block = 2 * level_at(place) + column
 
                 @pl.when(block != me)
                 def _():
-                    return_copy(block).start()
-                    prob_copy(block).start()
+                    return_copy(place, column, block).start()
+                    prob_copy(place, column, block).start()
 
                 @pl.when(block == me)
                 def _():
-                    back[rows(me, capacity), :] = result[rows(me, capacity), :]
-                    prob_in[me] = prob_out[me]
-
-            return carry
-
-        lax.fori_loop(0, levels, level_step, 0)
-
-    def partial_of(unit, quarter):
-        tensor, index = lax.div(unit, chunks), lax.rem(unit, chunks)
-        values = slots[1 - lax.div(tensor + 1, 2), :, cols(index)]
-        return contract_first(deltas[tensor, :, cols(quarter, share)], values)
-
-    def reduce_step(unit, carry):
-        @pl.when(unit < chunks)
-        def _():
-            cross_copy(1, level_at(levels - 1), lax.rem(unit, chunks)).wait_recv()
-
-        @pl.when(unit == chunks)
-        def _():
-            def last_step(part, inner):
-                backward_part(levels - 1, part, False)
-                return inner
-
-            lax.fori_loop(0, parts, last_step, 0)
-
-        @pl.when(unit == chunks + 1)
-        def _():
-            send_back()
-
-        slot = lax.rem(unit, 2)
-
-        @pl.when(unit >= 2)
-        def _():
-            pass_copy(unit - 2).wait_send()
-            keep_copy(unit - 2).wait_send()
-
-        near_out[slot] = partial_of(unit, diagonal).astype(jnp.bfloat16)
-        pass_copy(unit).start()
-        passed = partial_of(unit, far)
-        pass_copy(unit).wait_recv()
-        near_in[unit] = (passed + near_in[unit].astype(jnp.float32)).astype(jnp.bfloat16)
-        far_copy(unit).start()
-        keep_out[slot] = partial_of(unit, near).astype(jnp.bfloat16)
+                    back[rows(me, capacity), :] = result[rows(2 * place + column, capacity), :]
+                    prob_in[me] = prob_out[place, column]
+
+    period = 4 * chunks
+
+    def main_step(step, carry):
+        @pl.when(step == 2 * chunks)
+        def _():
+            for hop in range(1, ep_size):
+                meta_arrival(hop).wait_recv()
+            for which in range(2):
+                table_copy(which).start()
+            for load in loads:
+                load.wait()
+
+        @pl.when(step < 2 * period)
+        def _():
+            item = lax.div(step, chunks)
+            event(lax.rem(item, 2), lax.div(item, 2), lax.rem(step, chunks))
+
+        late = step - chunks - 1
+
+        @pl.when((late >= 0) & (lax.rem(late + period, chunks) == 0))
+        def _():
+            item = lax.div(late, chunks)
+
+            @pl.when(item < 2 * levels)
+            def _():
+                share_slots(lax.rem(item, 2), lax.div(item, 2))
+
+        for number, task in enumerate((forward_part, backward_part, return_part)):
+            since = step - (3 + number) * chunks - 1
+
+            @pl.when((since >= 0) & (lax.rem(since + 2 * period, period) < chunks))
+            def _():
+                task(2 * lax.div(since, period), 2, lax.rem(since, period))
+
+        return carry
+
+    lax.fori_loop(0, 2 * period + 2 * chunks + 1, main_step, 0)
+
+    def keep_step(unit, carry):
+        total = partial_of(unit, near).astype(jnp.bfloat16)
+
+        @pl.when(unit >= 1)
+        def _():
+            keep_copy(unit - 1).wait_send()
+
+        keep_out[...] = total
         keep_copy(unit).start()
         return carry
 
-    lax.fori_loop(0, units, reduce_step, 0)
+    def partial_of(unit, quarter):
+        return contract_first(deltas[unit, :, cols(quarter, share)], slots[1 - lax.div(unit + 1, 2)])
+
+    def far_partial(unit, half):
+        return contract_first(far_deltas[unit], far_slots[1 - lax.div(unit + 1, 2), half])
+
+    def pull(tensor, half):
+        for inner in range(2):
+            for column in range(2):
+                slot_copy(tensor, 2 * half + inner, column).wait_recv()
+            side_copy(tensor, 2 * half + inner).start()
+
+    def settle(tensor, half):
+        for inner in range(2):
+            side_copy(tensor, 2 * half + inner).wait_recv()
+
+    def far_forward(half):
+        for which in range(2):
+            for inner in range(2):
+                for column in range(2):
+                    base = which * pair + inner * group + column * capacity
+                    table = far_meta[which, 2 * level_at(2 * half + inner) + column]
+                    far_weight[base : base + capacity, :] = weight_of(table)
+        entries = far_slots[0, half]
+        gate_pre = contract_last(entries, w_gate[rows(rep, share), :])
+        up_pre = contract_last(entries, w_up[rows(rep, share), :])
+        gated, slope, activated = activate(gate_pre, up_pre)
+        far_deltas[1] = slope.astype(jnp.bfloat16)
+        far_deltas[2] = gated.astype(jnp.bfloat16)
+        far_deltas[0] = (activated * far_weight[...]).astype(jnp.bfloat16)
+
+    def far_backward(half):
+        back_proj = contract_last(far_slots[1, half], w_down[rows(rep, share), :])
+        act_delta = far_weight[...] * back_proj
+        for kind in (1, 2):
+            far_deltas[kind] = (act_delta * far_deltas[kind]).astype(jnp.bfloat16)
 
     def combine():
         for step in range(1, ep_size):
@@ -625,22 +633,49 @@
                 total = total + jnp.where(found, prob_in[expert][:1], 0.0)
             prob_ref[k : k + 1, :] = as_row(scale_col[...] * jnp.sum(total, axis=1, keepdims=True))
 
-    def finish_step(unit, carry):
-        @pl.when(unit == units - 2)
-        def _():
-            combine()
-
-        total = partial_of(unit, rep)
-        keep_copy(unit).wait_recv()
-        total = total + keep_in[unit].astype(jnp.float32)
-        far_copy(unit).wait_recv()
-        tensor, index = lax.div(unit, chunks), lax.rem(unit, chunks)
-        grads_ref[tensor, :, cols(index)] = (total + far_in[unit].astype(jnp.float32)).astype(
-            jnp.bfloat16
-        )
+    def far_step(half, carry):
+        @pl.when(half == 0)
+        def _():
+            pull(0, 0)
+            pull(1, 0)
+            for which in range(2):
+                table_copy(which).wait_recv()
+            lax.fori_loop(0, units, keep_step, 0)
+
+        settle(0, half)
+        far_forward(half)
+
+        settle(1, half)
+        far_backward(half)
+
+        @pl.when((half == 0) & (middle == 1))
+        def _():
+            send_back(2, 2)
+
+        def grads_step(unit, inner):
+            total = far_partial(unit, half)
+
+            @pl.when((half == 0) & (unit > 0))
+            def _():
+                pull(unit - 1, 1)
+
+            @pl.when(half == 0)
+            def _():
+                first = total + partial_of(unit, rep)
+                keep_copy(unit).wait_recv()
+                grads_ref[unit] = (first + keep_in[unit].astype(jnp.float32)).astype(jnp.bfloat16)
+
+            @pl.when(half == 1)
+            def _():
+                grads_ref[unit] = (total + grads_ref[unit].astype(jnp.float32)).astype(jnp.bfloat16)
+
+            return inner
+
+        lax.fori_loop(0, units, grads_step, 0)
         return carry
 
-    lax.fori_loop(0, units, finish_step, 0)
+    lax.fori_loop(0, 2, far_step, 0)
+    combine()
 
     for tensor in range(2):
         for index in range(chunks):
@@ -652,18 +687,26 @@
                 relay_copy(tensor, 1, index).wait_send()
                 relay_copy(tensor, 3, index).wait_send()
 
-            for level in range(levels):
-                cross_copy(tensor, level, index).wait_send()
+            for place in range(2, levels):
+                cross_copy(tensor, place, index).wait_send()
+        for place in range(levels):
+            for column in range(2):
+                slot_copy(tensor, place, column).wait_send()
+            side_copy(tensor, place).wait_send()
     for step in range(1, ep_size):
         meta_copy(step).wait_send()
-        peer = lax.rem(me + step, ep_size)
-        return_copy(peer).wait_send()
-        prob_copy(peer).wait_send()
-    for unit in (units - 2, units - 1):
-        pass_copy(unit).wait_send()
-        keep_copy(unit).wait_send()
-    for unit in range(units):
-        far_copy(unit).wait_send()
+    for place in range(levels):
+        for column in range(2):
+            block = 2 * level_at(place) + column
+
+            @pl.when(block != me)
+            def _():
+                return_copy(place, column, block).wait_send()
+                prob_copy(place, column, block).wait_send()
+
+    keep_copy(units - 1).wait_send()
+    for which in range(2):
+        table_copy(which).wait_send()
 
 
 def fused_body(
@@ -675,10 +718,11 @@
     hidden = gate_weight.shape[1]
     capacity = 5 * top * tok_rows // (4 * ep_size)
     slot_rows = ep_size * capacity
+    pair = slot_rows // 2
     chunk = width // 3
-    chunks, parts, levels = width // chunk, hidden // chunk, ep_size // 2
+    chunks, levels = width // chunk, ep_size // 2
     share = hidden // dp_size
-    units = 3 * chunks
+    units = 3
     bf16, f32 = jnp.bfloat16, jnp.float32
     vmem, dma = pltpu.VMEM, pltpu.SemaphoreType.DMA
     in_vmem = pl.BlockSpec(memory_space=pltpu.VMEM)
@@ -687,29 +731,29 @@
         vmem((hidden, width), bf16), vmem((hidden, width), bf16), vmem((hidden, width), bf16),
         vmem((2, levels, chunks, tok_rows, chunk), bf16),
         vmem((2, slot_rows, width), bf16),
-        vmem((2, levels, chunks, capacity, chunk), bf16),
+        vmem((2, 2, chunks, capacity, chunk), bf16),
         vmem((3, slot_rows, hidden), bf16),
-        vmem((parts, 2 * capacity, chunk), f32),
-        vmem((parts, 2 * capacity, chunk), f32),
-        vmem((parts, 2 * capacity, chunk), f32),
-        vmem((2 * capacity, 1), f32),
-        vmem((parts, 2 * capacity, 1), f32),
+        vmem((chunks, pair, chunk), bf16),
+        vmem((pair, 1), f32),
+        vmem((chunks, pair, 1), f32),
         vmem((ep_size, 2 * top, tok_rows), f32),
         vmem((top, tok_rows, 1), f32),
         vmem((tok_rows, 1), f32),
-        vmem((2, share, chunk), bf16),
-        vmem((units, share, chunk), bf16),
-        vmem((units, share, chunk), bf16),
-        vmem((2, share, chunk), bf16),
-        vmem((units, share, chunk), bf16),
+        vmem((share, width), bf16),
+        vmem((units, share, width), bf16),
         vmem((slot_rows, width), bf16),
         vmem((slot_rows, width), bf16),
+        vmem((levels, 2, 8, tok_rows), f32),
         vmem((ep_size, 8, tok_rows), f32),
-        vmem((ep_size, 8, tok_rows), f32),
+        vmem((2, 2, 2 * pair, width), bf16),
+        vmem((3, 2 * pair, share), bf16),
+        vmem((2 * pair, 1), f32),
+        vmem((2, ep_size, 2 * top, tok_rows), f32),
         dma((3,)), dma((2, 2, chunks)), dma((2, 2, chunks)), dma((2, levels, chunks)),
         dma((2, levels, chunks)), dma((2, levels, chunks)), dma((ep_size,)), dma((ep_size,)),
-        dma((units,)), dma((units,)), dma((units,)), dma((units,)), dma((units,)), dma((units,)),
-        dma((ep_size,)), dma((ep_size,)), dma((ep_size,)), dma((ep_size,)),
+        dma((units,)), dma((units,)), dma((levels, 2)), dma((ep_size,)), dma((levels, 2)),
+        dma((ep_size,)), dma((2, levels, 2)), dma((2, levels, 2)), dma((2, levels)), dma((2, levels)),
+        dma((2,)), dma((2,)),
     ]
     input_grad, prob_grad, grads = pl.pallas_call(
         functools.partial(fused_kernel, ep_size, dp_size, capacity, chunk),

time: 164 us -> 129 us (0.79); the launches traced: 161 us -> 129 us
  Pallas kernels: 155 us -> 123 us
    pallas_call x1, Pallas kernels: 155 us -> 123 us  [fused_body(): pl.pallas_call(functools.partial(fused_kernel, ep_size, dp_size, capacity...]
where the time goes in v2:
time: 129 us
  Pallas kernels  123 us (95%)
  local copies, waits for them, and re-layouts  5.23 us (4%)
    pallas_call x1, Pallas kernels, fused_body(): pl.pallas_call(functools.partial(fused_kernel, ep_size, dp_size, capacity...  123 us
    slice x1, local copies, waits for them, and re-layouts, fused_body(): grads[0][None]  3.9 us

profile of v2, /device:TPU:4, one launch (start us, length us, event | category | flops | bytes accessed | tf_op | source)
XLA Modules:
  0.0 128.6 jit_solution(8122171577246683263)
XLA Ops:
  0.6 122.7 %fused_step.1 = (bf16[128,1536]{1,0:T(8,128)(2,1)}, f32[4,128]{1,0:T(4,128)}, bf16[3,384,1536]{2,1,0:T(8,128)(2,1)}) custom-call(bf16[128,1536]{1,0:T(8,128)(2,1)} %tokens_ref.1, f32[128,1536]{1,0:T(8,128)} %grad_ref.1, f32[4,128]{1,0:T(4,128)} %bitcast.3, s32[4,128]{1,0:T(4,128)} %bitcast.4, s32[1,128]{1,0:T(1,128)} %prio_ref.1, s32[8]{0:T(128)} %caps_ref.1, ...), custom_call_target="tpu_custom_call" | custom-call | tf_op jit(solution)/shard_map/fused_step/pallas_call | solution.py:758
  123.3 0.0 copy-start
  123.4 0.0 copy-start.1
  123.4 3.9 %fusion = (bf16[1,384,1536]{2,1,0:T(8,128)(2,1)}, bf16[1,384,1536]{2,1,0:T(8,128)(2,1)}, bf16[1,384,1536]{2,1,0:T(8,128)(2,1)}) fusion(bf16[3,384,1536]{2,1,0:T(8,128)(2,1)} %get-tuple-element.10), kind=kLoop, calls=%fused_computation | loop fusion | bytes 7077888 | tf_op jit(solution)/shard_map/slice | solution.py:775
  127.3 0.0 copy-done
  127.3 0.7 copy.16
  128.0 0.0 copy-done.1
  128.0 0.6 copy.17
Async XLA Ops:
  123.3 3.9 %copy-start = (bf16[128,1536]{1,0:T(8,128)(2,1)S(1)}, bf16[128,1536]{1,0:T(8,128)(2,1)}, u32[]{:S(2)}) copy-start(bf16[128,1536]{1,0:T(8,128)(2,1)} %get-tuple-element.19) | copy-start | bytes 1179652
  123.4 4.7 %copy-start.1 = (f32[4,128]{1,0:T(4,128)S(1)}, f32[4,128]{1,0:T(4,128)}, u32[]{:S(2)}) copy-start(f32[4,128]{1,0:T(4,128)} %get-tuple-element.9) | copy-start | bytes 6148

commit v3 on v2

--- a/solution.py
+++ b/solution.py
@@ -291,7 +291,7 @@
 
     def keep_copy(unit):
         return remote(
-            keep_out, keep_in.at[unit], keep_send.at[unit], keep_recv.at[unit],
+            keep_out.at[lax.rem(unit, 2)], keep_in.at[unit], keep_send.at[unit], keep_recv.at[unit],
             {"dp": near},
         )
 
@@ -564,11 +564,11 @@
     def keep_step(unit, carry):
         total = partial_of(unit, near).astype(jnp.bfloat16)
 
-        @pl.when(unit >= 1)
-        def _():
-            keep_copy(unit - 1).wait_send()
-
-        keep_out[...] = total
+        @pl.when(unit >= 2)
+        def _():
+            keep_copy(unit - 2).wait_send()
+
+        keep_out[lax.rem(unit, 2)] = total
         keep_copy(unit).start()
         return carry
 
@@ -704,9 +704,37 @@
                 return_copy(place, column, block).wait_send()
                 prob_copy(place, column, block).wait_send()
 
-    keep_copy(units - 1).wait_send()
+    for step in (1, 2):
+        keep_copy(units - step).wait_send()
     for which in range(2):
         table_copy(which).wait_send()
+
+
+def emit_kernel(input_in, prob_in, grads_in, *refs):
+    outs, (stage_input, stage_prob, stage_grads, load_sem, store_sem) = refs[:5], refs[5:]
+    half = grads_in.shape[1] // 2
+    moves = [(input_in, stage_input, outs[0]), (prob_in, stage_prob, outs[1])]
+    for target, tensor in ((outs[2], 1), (outs[3], 2), (outs[4], 0)):
+        for part in range(2):
+            span = pl.ds(part * half, half)
+            moves.append(
+                (grads_in.at[tensor, span], stage_grads.at[tensor, span], target.at[0, span])
+            )
+    loads = [
+        pltpu.make_async_copy(source, stage, load_sem.at[i])
+        for i, (source, stage, _) in enumerate(moves)
+    ]
+    stores = [
+        pltpu.make_async_copy(stage, target, store_sem.at[i])
+        for i, (_, stage, target) in enumerate(moves)
+    ]
+    for load in loads:
+        load.start()
+    for load, store in zip(loads, stores):
+        load.wait()
+        store.start()
+    for store in stores:
+        store.wait()
 
 
 def fused_body(
@@ -739,7 +767,7 @@
         vmem((ep_size, 2 * top, tok_rows), f32),
         vmem((top, tok_rows, 1), f32),
         vmem((tok_rows, 1), f32),
-        vmem((share, width), bf16),
+        vmem((2, share, width), bf16),
         vmem((units, share, width), bf16),
         vmem((slot_rows, width), bf16),
         vmem((slot_rows, width), bf16),
@@ -772,7 +800,23 @@
     )(
         tokens, grad_out, probs.T, expert_ids.T, priority, cap_counts, gate_weight, up_weight, down_weight
     )
-    return input_grad, prob_grad.T, grads[1][None], grads[2][None], grads[0][None]
+    weight_shape = jax.ShapeDtypeStruct((1, share, width), bf16)
+    outs = pl.pallas_call(
+        emit_kernel,
+        out_shape=(
+            jax.ShapeDtypeStruct(input_grad.shape, bf16),
+            jax.ShapeDtypeStruct(prob_grad.shape, f32),
+            weight_shape, weight_shape, weight_shape,
+        ),
+        in_specs=[anywhere] * 3,
+        out_specs=[anywhere] * 5,
+        scratch_shapes=[
+            vmem(input_grad.shape, bf16), vmem(prob_grad.shape, f32), vmem(grads.shape, bf16),
+            dma((8,)), dma((8,)),
+        ],
+        name="emit",
+    )(input_grad, prob_grad, grads)
+    return outs[0], outs[1].T, outs[2], outs[3], outs[4]
 
 
 def on_device(*arrays):

time: 129 us -> 124 us (0.961)
  local copies, waits for them, and re-layouts: 5.23 us -> 0 us
    slice x1 -> x0, local copies, waits for them, and re-layouts: 3.9 us -> none  [fused_body(): grads[0][None]]
    pallas_call x0 -> x1, Pallas kernels: none -> 3.49 us  [fused_body(): pl.pallas_call(emit_kernel, out_shape=(jax.ShapeDtypeStruct(input_grad.sh...]
    pallas_call x1, Pallas kernels: 123 us -> 120 us  [fused_body(): pl.pallas_call(functools.partial(fused_kernel, ep_size, dp_size, capacity...]
    unnamed x6 -> x0, local copies, waits for them, and re-layouts: 1.33 us -> none
where the time goes in v3:
time: 124 us
  Pallas kernels  124 us (100%)
    pallas_call x1, Pallas kernels, fused_body(): pl.pallas_call(functools.partial(fused_kernel, ep_size, dp_size, capacity...  120 us
    pallas_call x1, Pallas kernels, fused_body(): pl.pallas_call(emit_kernel, out_shape=(jax.ShapeDtypeStruct(input_grad.sh...  3.49 us

profile of v3, /device:TPU:4, one launch (start us, length us, event | category | flops | bytes accessed | tf_op | source)
XLA Modules:
  0.0 124.3 jit_solution(693575796108699788)
XLA Ops:
  0.6 120.2 %fused_step.1 = (bf16[128,1536]{1,0:T(8,128)(2,1)}, f32[4,128]{1,0:T(4,128)}, bf16[3,384,1536]{2,1,0:T(8,128)(2,1)}) custom-call(bf16[128,1536]{1,0:T(8,128)(2,1)} %tokens_ref.1, f32[128,1536]{1,0:T(8,128)} %grad_ref.1, f32[4,128]{1,0:T(4,128)} %bitcast.3, s32[4,128]{1,0:T(4,128)} %bitcast.4, s32[1,128]{1,0:T(1,128)} %prio_ref.1, s32[8]{0:T(128)} %caps_ref.1, ...), custom_call_target="tpu_custom_call" | custom-call | tf_op jit(solution)/shard_map/fused_step/pallas_call | solution.py:786
  120.8 3.5 %emit.1 = (bf16[128,1536]{1,0:T(8,128)(2,1)}, f32[4,128]{1,0:T(4,128)}, bf16[1,384,1536]{2,1,0:T(8,128)(2,1)}, bf16[1,384,1536]{2,1,0:T(8,128)(2,1)}, bf16[1,384,1536]{2,1,0:T(8,128)(2,1)}) custom-call(bf16[128,1536]{1,0:T(8,128)(2,1)} %get-tuple-element.13.input_in, f32[4,128]{1,0:T(4,128)} %get-tuple-element.14.prob_in, ...), custom_call_target="tpu_custom_call" | custom-call | tf_op jit(solution)/shard_map/emit/pallas_call | solution.py:804
